TPU v7x, 32 devices: a whole 2x2x4 slice. The times are simulated.
32 devices in a mesh: rep: 4 (over x, core), dp: 4 (over z), tp: 2 (over y).
Axes of the slice: x: 2, y: 2, z: 4, core: 2. Of those that a mesh axis runs over, the one named last changes fastest.
Arguments:
- hidden: bfloat16 [4, 512, 14336], P('rep', None, 'tp'), may hold values from -6 to 6
- down_weight: bfloat16 [14336, 8192], P('tp', 'dp'), may hold values from -0.046875 to 0.046875
- out_grad: bfloat16 [4, 512, 8192], P('rep', 'tp', 'dp'), may hold values from -6 to 6
- pseudo_grad: bfloat16 [4, 14336, 8192], P('rep', 'tp', 'dp'), may hold values from -6 to 6
- momentum: float32 [14336, 8192], P(('tp', 'rep'), 'dp'), may hold values from -6 to 6
Outputs:
- layer_out: bfloat16 [4, 512, 8192], P('rep', 'tp', 'dp')
- hidden_grad: bfloat16 [4, 512, 14336], P('rep', 'dp', 'tp')
- new_momentum: float32 [14336, 8192], P(('tp', 'rep'), 'dp')
- outer_step: bfloat16 [14336, 8192], P('tp', 'dp')
All inputs are finite; a program needn't handle non-finite values.
Results may differ from a plain program's by a relative error of at most 0.017.
Values may be sent and summed in bfloat16 or wider, within the bound.
A program may use at most 256 MiB of HBM per device.

v0:
```python
import jax
import jax.numpy as jnp
from jax import lax
from jax.sharding import PartitionSpec as P

outer_rate = 0.7
momentum_rate = 0.9


def per_device(hidden, down_weight, out_grad, pseudo_grad, momentum):
    token_rows = hidden[0]
    local_grads = out_grad[0]
    row_block = token_rows
    layer_out = lax.psum_scatter(
        jnp.dot(row_block, down_weight, preferred_element_type=jnp.float32).astype(jnp.bfloat16),
        "tp",
        scatter_dimension=0,
        tiled=True,
    )
    all_grads = lax.all_gather(local_grads, "tp", axis=0, tiled=True)
    row_block = all_grads
    hidden_grad = lax.psum_scatter(
        lax.dot_general(
            row_block, down_weight, (((1,), (1,)), ((), ())), preferred_element_type=jnp.float32
        ).astype(jnp.bfloat16),
        "dp",
        scatter_dimension=0,
        tiled=True,
    )
    replicas = lax.axis_size("rep")
    replica_terms = pseudo_grad[0].astype(jnp.float32)
    average = (
        lax.psum_scatter(
            replica_terms.astype(jnp.bfloat16), "rep", scatter_dimension=0, tiled=True
        ).astype(jnp.float32)
        / replicas
    )
    new_momentum = momentum_rate * momentum + average
    step_share = (outer_rate * (average + momentum_rate * new_momentum)).astype(jnp.bfloat16)
    outer_step = lax.all_gather(step_share, "rep", axis=0, tiled=True)
    return (layer_out[None], hidden_grad[None], new_momentum, outer_step)


def solution(mesh):
    return jax.shard_map(
        per_device,
        mesh=mesh,
        in_specs=(
            P("rep", None, "tp"),
            P("tp", "dp"),
            P("rep", "tp", "dp"),
            P("rep", "tp", "dp"),
            P(("tp", "rep"), "dp"),
        ),
        out_specs=(
            P("rep", "tp", "dp"),
            P("rep", "dp", "tp"),
            P(("tp", "rep"), "dp"),
            P("tp", "dp"),
        ),
        check_vma=False,
    )
```

profile of v0, /device:TPU:0, one launch (start us, length us, event | category | flops | bytes accessed | tf_op | source)
XLA Modules:
  0.0 610.3 jit_solution(9170276419713844570)
XLA Ops:
  8.0 0.0 reduce-scatter.8.cloned.1.call-start
  8.0 0.7 reduce-scatter.8.cloned.1.call-update
  8.7 0.0 all-gather.6.cloned.1.call-start
  8.8 0.5 all-gather.6.cloned.1.call-update
  9.3 0.0 all-gather.4.cloned.1.call-start
  9.4 214.8 %reduce-scatter.8.cloned.1.call-done = bf16[1792,2048]{1,0:T(8,128)(2,1)} async-done(((bf16[7168,2048]{1,0:T(8,128)(2,1)}), bf16[1792,2048]{1,0:T(8,128)(2,1)}) %reduce-scatter.8.cloned.1.call-update) | async-done | bytes 7340048 | tf_op jit(solution)/shard_map/reduce_scatter | solution.py:33
  224.1 15.4 %multiply_convert_fusion = (bf16[1792,2048]{1,0:T(8,128)(2,1)}, f32[1792,2048]{1,0:T(8,128)}) fusion(bf16[1792,2048]{1,0:T(8,128)(2,1)} %reduce-scatter.8.cloned.1.call-done, f32[1792,2048]{1,0:T(8,128)} %param.9), kind=kLoop, calls=%fused_computation | loop fusion | flops 29360128 | bytes 44040192 | tf_op jit(solution)/shard_map/convert_element_type | solution.py:39
  239.5 0.0 all-gather.4.cloned.1.call-update
  239.5 0.0 reduce-scatter.4.cloned.1.call-start
  239.6 24.8 %fusion.3 = bf16[512,2048]{1,0:T(8,128)(2,1)} fusion(bf16[7168,2048]{1,0:T(8,128)(2,1)} %param.6, bf16[1,512,7168]{2,1,0:T(8,128)(2,1)} %param.5), kind=kOutput, calls=%fused_computation.6 | convolution fusion | flops 15033434112 | bytes 38797312 | tf_op jit(solution)/shard_map/dot_general | solution.py:15
  264.4 0.0 reduce-scatter.4.cloned.1.call-update
  264.4 0.0 reduce-scatter.6.cloned.1.call-start
  264.5 0.0 all-gather.6.cloned.1.call-done
  264.5 23.1 %convolution_convert_fusion = bf16[512,7168]{1,0:T(8,128)(2,1)} fusion(bf16[7168,2048]{1,0:T(8,128)(2,1)} %param.6, bf16[1,512,2048]{2,1,0:T(8,128)(2,1)} %all-gather.6.cloned.1.call-done), kind=kOutput, calls=%fused_computation.3 | convolution fusion | flops 15036055552 | bytes 38797312 | tf_op jit(solution)/shard_map/dot_general | solution.py:23
  287.6 0.0 reduce-scatter.6.cloned.1.call-update
  287.6 129.9 %all-gather.4.cloned.1.call-done = bf16[7168,2048]{1,0:T(8,128)(2,1)} async-done(((bf16[1792,2048]{1,0:T(8,128)(2,1)}), bf16[7168,2048]{1,0:T(8,128)(2,1)}) %all-gather.4.cloned.1.call-update) | async-done | bytes 29360144 | tf_op jit(solution)/shard_map/all_gather | solution.py:40
  417.5 34.5 %reduce-scatter.4.cloned.1.call-done = bf16[256,2048]{1,0:T(8,128)(2,1)} async-done(((bf16[512,2048]{1,0:T(8,128)(2,1)}), bf16[256,2048]{1,0:T(8,128)(2,1)}) %reduce-scatter.4.cloned.1.call-update) | async-done | bytes 1048592 | tf_op jit(solution)/shard_map/reduce_scatter | solution.py:14
  452.0 130.6 %reduce-scatter.6.cloned.1.call-done = bf16[128,7168]{1,0:T(8,128)(2,1)} async-done(((bf16[512,7168]{1,0:T(8,128)(2,1)}), bf16[128,7168]{1,0:T(8,128)(2,1)}) %reduce-scatter.6.cloned.1.call-update) | async-done | bytes 1835024 | tf_op jit(solution)/shard_map/reduce_scatter | solution.py:22
  582.7 20.1 %copy.10 = bf16[7168,2048]{1,0:T(8,128)(2,1)} copy(bf16[7168,2048]{1,0:T(8,128)(2,1)} %all-gather.4.cloned.1.call-done) | data formatting | bytes 58720256
Async XLA Ops:
  8.0 216.1 %reduce-scatter.8.cloned.1.call-start = ((), (), s32[]{:S(2)}) async-start(), calls=%async_computation.5 | async-start | bytes 36700160 | tf_op jit(solution)/shard_map/reduce_scatter | solution.py:33
  8.7 255.8 %all-gather.6.cloned.1.call-start = ((), (), s32[]{:S(2)}) async-start(), calls=%async_computation.7 | async-start | bytes 3145728 | tf_op jit(solution)/shard_map/all_gather | solution.py:20
  9.3 408.2 %all-gather.4.cloned.1.call-start = ((), (), s32[]{:S(2)}) async-start(), calls=%async_computation.6 | async-start | bytes 36700160 | tf_op jit(solution)/shard_map/all_gather | solution.py:40
  239.5 212.5 %reduce-scatter.4.cloned.1.call-start = ((), (), s32[]{:S(2)}) async-start(), calls=%async_computation.3 | async-start | bytes 3145728 | tf_op jit(solution)/shard_map/reduce_scatter | solution.py:14
  264.4 318.3 %reduce-scatter.6.cloned.1.call-start = ((), (), s32[]{:S(2)}) async-start(), calls=%async_computation.4 | async-start | bytes 9175040 | tf_op jit(solution)/shard_map/reduce_scatter | solution.py:22
Sparse Core Ops, SparseCore 0:
  11.4 212.6 reduce-scatter.7
Sparse Core Ops, SparseCore 1:
  10.8 35.7 all-gather.5
  239.6 177.8 all-gather.3
  420.2 31.8 reduce-scatter.3
  454.9 127.7 reduce-scatter.5
where the time goes:
time: 610 us
  waiting for transfers between devices  511 us (84%)
  matrix products  47.9 us (8%)
  local copies, waits for them, and re-layouts  20.1 us (3%)
  between operations  15.7 us (3%)
  other arithmetic  15.4 us (3%)
    reduce_scatter x1, waiting for transfers between devices, per_device(): lax.psum_scatter(replica_terms.astype(jnp.bfloat16), 'rep', scatter_dimen...  215 us
    reduce_scatter x1, waiting for transfers between devices, per_device(): lax.psum_scatter(lax.dot_general(row_block, down_weight, (((1,), (1,)), (...  131 us
    all_gather x1, waiting for transfers between devices, per_device(): outer_step = lax.all_gather(step_share, 'rep', axis=0, tiled=True)  130 us
    reduce_scatter x1, waiting for transfers between devices, per_device(): lax.psum_scatter(jnp.dot(row_block, down_weight, preferred_element_type=j...  34.5 us
    dot_general x1, matrix products, per_device(): jnp.dot(row_block, down_weight, preferred_element_type=jnp.float32)  24.8 us
    dot_general x1, matrix products, per_device(): lax.dot_general(row_block, down_weight, (((1,), (1,)), ((), ())), preferr...  23.1 us
    unnamed x1, local copies, waits for them, and re-layouts  20.1 us
    convert_element_type x1, other arithmetic, per_device(): (outer_rate * (average + momentum_rate * new_momentum)).astype(jnp.bfloat16)  15.4 us
  transfers between devices with their start and end apart: 5, of which 4 were waited for; matrix products, arithmetic and copies ran while one was open for 10% of the time, Pallas kernels for 0%

commit v1 on v0

--- a/solution.py
+++ b/solution.py
@@ -5,6 +5,17 @@
 
 outer_rate = 0.7
 momentum_rate = 0.9
+
+
+def around_the_ring(x, mesh_axis, d):
+    count = lax.axis_size(mesh_axis)
+    forward = [(i, (i + 1) % count) for i in range(count)]
+    parts = [x]
+    for stride in range(1, count):
+        parts = [lax.ppermute(parts[0], mesh_axis, forward), *parts]
+    whole = jnp.concatenate(parts, axis=d)
+    turn = (lax.axis_index(mesh_axis) + 1) * parts[-1].shape[d]
+    return jnp.roll(whole, turn, axis=d)
 
 
 def per_device(hidden, down_weight, out_grad, pseudo_grad, momentum):
@@ -37,7 +48,7 @@
     )
     new_momentum = momentum_rate * momentum + average
     step_share = (outer_rate * (average + momentum_rate * new_momentum)).astype(jnp.bfloat16)
-    outer_step = lax.all_gather(step_share, "rep", axis=0, tiled=True)
+    outer_step = around_the_ring(step_share, "rep", 0)
     return (layer_out[None], hidden_grad[None], new_momentum, outer_step)
 
 

time: 610 us -> 569 us (0.933)
  waiting for transfers between devices: 511 us -> 415 us
  local copies, waits for them, and re-layouts: 20.1 us -> 77.5 us
    ppermute x0 -> x3, waiting for transfers between devices: none -> 199 us  [around_the_ring(): parts = [lax.ppermute(parts[0], mesh_axis, forward), *parts]]
    reduce_scatter x1, waiting for transfers between devices: 131 us -> 0.01 us  [per_device(): lax.psum_scatter(lax.dot_general(row_block, down_weight, (((1,), (1,)), (...]
    all_gather x1 -> x0, waiting for transfers between devices: 130 us -> none  [per_device(): outer_step = lax.all_gather(step_share, 'rep', axis=0, tiled=True)]
    reduce_scatter x1, waiting for transfers between devices: 34.5 us -> 0.01 us  [per_device(): lax.psum_scatter(jnp.dot(row_block, down_weight, preferred_element_type=j...]
    unnamed x1 -> x13, local copies, waits for them, and re-layouts: 20.1 us -> 52.7 us
    dynamic_slice x0 -> x1, local copies, waits for them, and re-layouts: none -> 20.5 us  [around_the_ring(): return jnp.roll(whole, turn, axis=d)]
  transfers between devices with their start and end apart: 5 -> 7, of which waited for: 4 -> 4; matrix products, arithmetic and copies ran while one was open for 10% -> 21% of each run, Pallas kernels for 0% -> 0%
where the time goes in v1:
time: 569 us; the launch traced here: 568 us
  waiting for transfers between devices  415 us (73%)
  local copies, waits for them, and re-layouts  77.5 us (14%)
  matrix products  46.6 us (8%)
  between operations  15.7 us (3%)
  other arithmetic  13.4 us (2%)
    reduce_scatter x1, waiting for transfers between devices, per_device(): lax.psum_scatter(replica_terms.astype(jnp.bfloat16), 'rep', scatter_dimen...  215 us
    ppermute x3, waiting for transfers between devices, around_the_ring(): parts = [lax.ppermute(parts[0], mesh_axis, forward), *parts]  199 us
    unnamed x13, local copies, waits for them, and re-layouts  52.7 us
    dot_general x1, matrix products, per_device(): jnp.dot(row_block, down_weight, preferred_element_type=jnp.float32)  23.8 us
    dot_general x1, matrix products, per_device(): lax.dot_general(row_block, down_weight, (((1,), (1,)), ((), ())), preferr...  22.8 us
    dynamic_slice x1, local copies, waits for them, and re-layouts, around_the_ring(): return jnp.roll(whole, turn, axis=d)  20.5 us
    convert_element_type x1, other arithmetic, per_device(): (outer_rate * (average + momentum_rate * new_momentum)).astype(jnp.bfloat16)  13.4 us
  transfers between devices with their start and end apart: 7, of which 4 were waited for; matrix products, arithmetic and copies ran while one was open for 21% of the time, Pallas kernels for 0%

profile of v1, /device:TPU:0, one launch (start us, length us, event | category | flops | bytes accessed | tf_op | source)
XLA Modules:
  0.0 568.4 jit_solution(3590842486752241648)
XLA Ops:
  8.0 0.0 reduce-scatter.8.cloned.1.call-start
  8.0 0.7 reduce-scatter.8.cloned.1.call-update
  8.7 0.0 all-gather.3.cloned.1.call-start
  8.8 215.4 %reduce-scatter.8.cloned.1.call-done = bf16[1792,2048]{1,0:T(8,128)(2,1)} async-done(((bf16[7168,2048]{1,0:T(8,128)(2,1)}), bf16[1792,2048]{1,0:T(8,128)(2,1)}) %reduce-scatter.8.cloned.1.call-update) | async-done | bytes 7340048 | tf_op jit(solution)/shard_map/reduce_scatter | solution.py:44
  224.1 13.4 %multiply_convert_fusion = (bf16[1792,2048]{1,0:T(8,128)(2,1)S(1)}, f32[1792,2048]{1,0:T(8,128)}) fusion(bf16[1792,2048]{1,0:T(8,128)(2,1)} %reduce-scatter.8.cloned.1.call-done, f32[1792,2048]{1,0:T(8,128)} %param.9), kind=kLoop, calls=%fused_computation | loop fusion | flops 29360128 | bytes 44040192 | tf_op jit(solution)/shard_map/convert_element_type | solution.py:50
  237.6 0.0 copy-start
  237.6 3.0 copy-done
  240.6 0.0 collective-permute-start
  240.6 81.7 %collective-permute-done = bf16[1792,2048]{1,0:T(8,128)(2,1)} collective-permute-done((bf16[1792,2048]{1,0:T(8,128)(2,1)S(1)}, bf16[1792,2048]{1,0:T(8,128)(2,1)}, u32[]{:S(2)}, u32[]{:S(2)}) %collective-permute-start) | collective-permute-done | bytes 7340064 | tf_op jit(solution)/shard_map/ppermute | solution.py:15
  322.4 0.0 collective-permute-start.1
  322.4 0.0 all-gather.3.cloned.1.call-update
  322.4 0.0 reduce-scatter.4.cloned.1.call-start
  322.5 23.8 %fusion.3 = bf16[512,2048]{1,0:T(8,128)(2,1)} fusion(bf16[7168,2048]{1,0:T(8,128)(2,1)} %param.6, bf16[1,512,7168]{2,1,0:T(8,128)(2,1)} %param.5), kind=kOutput, calls=%fused_computation.6 | convolution fusion | flops 15033434112 | bytes 38797312 | tf_op jit(solution)/shard_map/dot_general | solution.py:26
  346.3 0.0 reduce-scatter.4.cloned.1.call-update
  346.3 0.0 reduce-scatter.6.cloned.1.call-start
  346.3 58.0 %collective-permute-done.1 = bf16[1792,2048]{1,0:T(8,128)(2,1)} collective-permute-done((bf16[1792,2048]{1,0:T(8,128)(2,1)}, bf16[1792,2048]{1,0:T(8,128)(2,1)}, u32[]{:S(2)}, u32[]{:S(2)}) %collective-permute-start.1) | collective-permute-done | bytes 7340064 | tf_op jit(solution)/shard_map/ppermute | solution.py:15
  404.3 0.0 collective-permute-start.2
  404.3 22.8 %convolution_convert_fusion = bf16[512,7168]{1,0:T(8,128)(2,1)} fusion(bf16[7168,2048]{1,0:T(8,128)(2,1)} %param.6, bf16[1,512,2048]{2,1,0:T(8,128)(2,1)} %all-gather.3.cloned.1.call-done), kind=kOutput, calls=%fused_computation.3 | convolution fusion | flops 15036055552 | bytes 38797312 | tf_op jit(solution)/shard_map/dot_general | solution.py:34
  427.1 0.0 reduce-scatter.6.cloned.1.call-update
  427.1 59.1 %collective-permute-done.2 = bf16[1792,2048]{1,0:T(8,128)(2,1)} collective-permute-done((bf16[1792,2048]{1,0:T(8,128)(2,1)}, bf16[1792,2048]{1,0:T(8,128)(2,1)}, u32[]{:S(2)}, u32[]{:S(2)}) %collective-permute-start.2) | collective-permute-done | bytes 7340064 | tf_op jit(solution)/shard_map/ppermute | solution.py:15
  486.3 7.4 %constant_dynamic-update-slice_fusion.7 = bf16[14336,2048]{1,0:T(8,128)(2,1)} fusion(bf16[1792,2048]{1,0:T(8,128)(2,1)} %collective-permute-done.2), kind=kLoop, calls=%fused_computation.15 | loop fusion | bytes 14680064
  493.7 7.7 %constant_dynamic-update-slice_fusion.6 = bf16[14336,2048]{1,0:T(8,128)(2,1)} fusion(bf16[14336,2048]{1,0:T(8,128)(2,1)} %constant_dynamic-update-slice_fusion.7, bf16[1792,2048]{1,0:T(8,128)(2,1)} %collective-permute-done.1), kind=kLoop, calls=%fused_computation.14 | loop fusion | bytes 14680064
  501.5 7.6 %constant_dynamic-update-slice_fusion.5 = bf16[14336,2048]{1,0:T(8,128)(2,1)} fusion(bf16[14336,2048]{1,0:T(8,128)(2,1)} %constant_dynamic-update-slice_fusion.6, bf16[1792,2048]{1,0:T(8,128)(2,1)} %collective-permute-done), kind=kLoop, calls=%fused_computation.13 | loop fusion | bytes 14680064
  509.1 0.0 slice-done
  509.1 0.0 slice-done.1
  509.1 4.4 constant_dynamic-update-slice_fusion.4
  513.4 7.6 %constant_dynamic-update-slice_fusion.3 = bf16[14336,2048]{1,0:T(8,128)(2,1)} fusion(bf16[14336,2048]{1,0:T(8,128)(2,1)} %constant_dynamic-update-slice_fusion.4, bf16[1792,2048]{1,0:T(8,128)(2,1)} %collective-permute-done.2), kind=kLoop, calls=%fused_computation.11 | loop fusion | bytes 14680064
  521.0 7.5 %constant_dynamic-update-slice_fusion.2 = bf16[14336,2048]{1,0:T(8,128)(2,1)} fusion(bf16[14336,2048]{1,0:T(8,128)(2,1)} %constant_dynamic-update-slice_fusion.3, bf16[1792,2048]{1,0:T(8,128)(2,1)} %collective-permute-done.1), kind=kLoop, calls=%fused_computation.10 | loop fusion | bytes 14680064
  528.5 7.5 %constant_dynamic-update-slice_fusion.1 = bf16[14336,2048]{1,0:T(8,128)(2,1)} fusion(bf16[14336,2048]{1,0:T(8,128)(2,1)} %constant_dynamic-update-slice_fusion.2, bf16[1792,2048]{1,0:T(8,128)(2,1)} %collective-permute-done), kind=kLoop, calls=%fused_computation.9 | loop fusion | bytes 14680064
  536.0 4.3 constant_dynamic-update-slice_fusion
  540.3 20.5 %constant_dynamic-slice_fusion = bf16[7168,2048]{1,0:T(8,128)(2,1)} fusion(bf16[14336,2048]{1,0:T(8,128)(2,1)} %constant_dynamic-update-slice_fusion, s32[]{:T(128)S(6)} %select_n.14), kind=kLoop, calls=%fused_computation.16 | loop fusion | bytes 58720260 | tf_op jit(solution)/shard_map/jit(_roll_dynamic)/dynamic_slice | solution.py:18
  560.8 0.0 reduce-scatter.6.cloned.1.call-done
  (5 shorter events, 0.0 us)
Async XLA Ops:
  8.0 216.1 %reduce-scatter.8.cloned.1.call-start = ((), (), s32[]{:S(2)}) async-start(), calls=%async_computation.5 | async-start | bytes 36700160 | tf_op jit(solution)/shard_map/reduce_scatter | solution.py:44
  8.7 395.6 %all-gather.3.cloned.1.call-start = ((), (), s32[]{:S(2)}) async-start(), calls=%async_computation.6 | async-start | bytes 3145728 | tf_op jit(solution)/shard_map/all_gather | solution.py:31
  237.6 3.0 copy-start
  240.6 81.7 %collective-permute-start = (bf16[1792,2048]{1,0:T(8,128)(2,1)S(1)}, bf16[1792,2048]{1,0:T(8,128)(2,1)}, u32[]{:S(2)}, u32[]{:S(2)}) collective-permute-start(bf16[1792,2048]{1,0:T(8,128)(2,1)S(1)} %get-tuple-element.4), channel_id=1, source_target_pairs={{0,8},{8,16},{16,24},{24,0},{1,9},{9,17},{17,25},{25,1},{2,10},{10... | collective-permute-start | bytes 22020104 | tf_op jit(solution)/shard_map/ppermute | solution.py:15
  322.4 82.0 %collective-permute-start.1 = (bf16[1792,2048]{1,0:T(8,128)(2,1)}, bf16[1792,2048]{1,0:T(8,128)(2,1)}, u32[]{:S(2)}, u32[]{:S(2)}) collective-permute-start(bf16[1792,2048]{1,0:T(8,128)(2,1)} %collective-permute-done), channel_id=1, source_target_pairs={{0,8},{8,16},{16,24},{24,0},{1,9},{9,17},{17,25},{25,1},{2,10},{10... | collective-permute-start | bytes 22020104 | tf_op jit(solution)/shard_map/ppermute | solution.py:15
  322.4 238.4 %reduce-scatter.4.cloned.1.call-start = ((), (), s32[]{:S(2)}) async-start(), calls=%async_computation.3 | async-start | bytes 3145728 | tf_op jit(solution)/shard_map/reduce_scatter | solution.py:25
  346.3 214.5 %reduce-scatter.6.cloned.1.call-start = ((), (), s32[]{:S(2)}) async-start(), calls=%async_computation.4 | async-start | bytes 9175040 | tf_op jit(solution)/shard_map/reduce_scatter | solution.py:33
  404.3 82.0 %collective-permute-start.2 = (bf16[1792,2048]{1,0:T(8,128)(2,1)}, bf16[1792,2048]{1,0:T(8,128)(2,1)}, u32[]{:S(2)}, u32[]{:S(2)}) collective-permute-start(bf16[1792,2048]{1,0:T(8,128)(2,1)} %collective-permute-done.1), channel_id=1, source_target_pairs={{0,8},{8,16},{16,24},{24,0},{1,9},{9,17},{17,25},{25,1},{2,10},{10... | collective-permute-start | bytes 22020104 | tf_op jit(solution)/shard_map/ppermute | solution.py:15
  493.7 15.4 %slice-start = ((s8[7340032]{0:T(1024)(128)(4,1)}), s8[4194304]{0:T(1024)(128)(4,1)S(1)}, s32[]{:S(2)}) async-start(s8[7340032]{0:T(1024)(128)(4,1)} %bitcast.13), calls=%async_computation.7 | async-start | bytes 8388608
  501.5 7.6 %slice-start.1 = ((s8[7340032]{0:T(1024)(128)(4,1)}), s8[3145728]{0:T(1024)(128)(4,1)S(1)}, s32[]{:S(2)}) async-start(s8[7340032]{0:T(1024)(128)(4,1)} %bitcast.13), calls=%async_computation.8 | async-start | bytes 6291456
Sparse Core Ops, SparseCore 0:
  11.4 212.6 reduce-scatter.7
Sparse Core Ops, SparseCore 1:
  322.5 34.1 all-gather.2
  359.3 31.8 reduce-scatter.3
  427.2 128.8 reduce-scatter.5
